TPU v7x, 32 devices: a whole 2x2x4 slice. The times are simulated.
32 devices in a mesh: group: 4 (over y, core), freq: 8 (over z, x).
Axes of the slice: x: 2, y: 2, z: 4, core: 2. Of those that a mesh axis runs over, the one named last changes fastest.
Arguments:
- spectra: bfloat16 [2048, 2, 16], P('freq', None, 'group'), may hold values from -6 to 6
- templates: bfloat16 [2048, 2, 2560], P('freq', None, 'group'), may hold values from -600 to 600
- valid_start: int32 [16], replicated, may hold values from 0 to 2048
Outputs:
- peaks: float32 [2560, 16], P('group')
All inputs are finite; a program needn't handle non-finite values.
Results may differ from a plain program's by a relative error of at most 0.0019.
Values may be sent and summed in bfloat16 or wider, within the bound.
A program may use at most 256 MiB of HBM per device.

v0:
```python
import functools
import math

import jax
import jax.numpy as jnp
import numpy as np
from jax import lax
from jax.experimental import pallas as pl
from jax.experimental.pallas import tpu as pltpu
from jax.sharding import PartitionSpec as P

LANES = 128
RADIX = 16
SUB = 8
SCALE = 1.1328125


def rotation(angle, row_axis, col_axis):
    cosine, sine = np.cos(angle), np.sin(angle)
    top = np.stack([cosine, -sine], col_axis)
    bottom = np.stack([sine, cosine], col_axis)
    return np.stack([top, bottom], row_axis)


def tables(bins):
    lags = 2 * bins
    inner = lags // RADIX
    a = np.arange(bins // RADIX)
    tau1 = np.arange(inner)
    angle = 2.0 * math.pi * ((tau1[:, None] * a[None, :]) % inner) / inner
    first = rotation(angle.reshape(inner // SUB, SUB, a.size), 1, 2)
    first = first.reshape(inner // SUB, 2, SUB, 2 * a.size)
    turn = 2.0 * math.pi * tau1.reshape(inner // SUB, SUB, 1) / lags
    turn = np.stack([np.cos(turn), np.sin(turn)], 0)
    b = np.arange(RADIX)
    angle = 2.0 * math.pi * ((b[:, None] * b[None, :]) % RADIX) / RADIX
    second = rotation(angle, 0, 2) * SCALE
    second = second.reshape(2 * RADIX, 2 * RADIX)
    second = np.kron(second, np.eye(SUB))
    return first.astype(np.float32), turn.astype(np.float32), second.astype(jnp.bfloat16)


def kernel(valid, r_ref, d_ref, base_ref, turn_ref, w2_ref, vs_ref, out_ref, work_ref, w1_ref, dexp_ref, y_ref):
    step = pl.program_id(0)
    width = out_ref.shape[2]
    parts, _, depth2, _ = r_ref.shape
    depth = depth2 // 2
    segs = d_ref.shape[3]
    per_tile = LANES // segs
    half = parts * depth
    rows2, cols2 = w2_ref.shape
    groups = y_ref.shape[0]
    inner = groups * SUB

    @pl.when(step == 0)
    def _():
        work_ref[...] = base_ref[...]

        @pl.loop(0, RADIX)
        def _(b):
            w1_ref[b] = work_ref[...].reshape(w1_ref.shape[1:]).astype(jnp.bfloat16)
            top, bottom = work_ref[:, 0], work_ref[:, 1]
            cosine, sine = turn_ref[0], turn_ref[1]
            work_ref[:, 0] = top * cosine - bottom * sine
            work_ref[:, 1] = bottom * cosine + top * sine

        seg_spread = (
            lax.broadcasted_iota(jnp.int32, (segs, LANES), 0)
            == lax.broadcasted_iota(jnp.int32, (segs, LANES), 1) // per_tile
        ).astype(jnp.bfloat16)

        @pl.loop(0, RADIX)
        def _(b):
            piece = d_ref[:, b].reshape(2 * half, segs)
            dexp_ref[b] = jnp.dot(piece, seg_spread, preferred_element_type=jnp.float32)

    lane = lax.broadcasted_iota(jnp.int32, (LANES, width), 1)
    wanted = step * (width // segs) + (lane // LANES) * per_tile + lane % per_tile
    pick = (lax.broadcasted_iota(jnp.int32, (LANES, width), 0) == wanted).astype(jnp.bfloat16)

    def split(x):
        x = x.reshape(parts, 2, depth, x.shape[1])
        return x[:, 0].reshape(half, -1), x[:, 1].reshape(half, -1)

    def first_stage(b, norm):
        bank = jnp.dot(
            r_ref[:, b].reshape(2 * half, LANES), pick, preferred_element_type=jnp.float32
        )
        h0, h1 = split(bank)
        d0, d1 = split(dexp_ref[b])
        d0 = jnp.concatenate([d0] * (width // LANES), 1)
        d1 = jnp.concatenate([d1] * (width // LANES), 1)
        square = h0 * h0 + h1 * h1
        norm = norm + jnp.sum(square.reshape(half // SUB, SUB, width), 0)
        cross = jnp.concatenate([h0 * d0 + h1 * d1, h0 * d1 - h1 * d0], 0).astype(jnp.bfloat16)
        y = jnp.dot(w1_ref[b], cross, preferred_element_type=jnp.float32)
        y_ref[:, b] = y.astype(jnp.bfloat16).reshape(groups, 2 * SUB, width)
        return norm

    norm = lax.fori_loop(
        0, RADIX, first_stage, jnp.zeros((SUB, width), jnp.float32), unroll=2
    )
    offset = lax.broadcasted_iota(jnp.int32, (SUB, width), 0) - vs_ref[...]
    row = lax.broadcasted_iota(jnp.int32, (RADIX, SUB, width), 0) * inner

    def second_stage(g, best):
        z = jnp.dot(
            w2_ref[...], y_ref[g].reshape(cols2, width), preferred_element_type=jnp.float32
        )
        re, im = z[: rows2 // 2], z[rows2 // 2 :]
        power = (re * re + im * im).reshape(RADIX, SUB, width)
        late = row + (offset + g * SUB)[None]
        inside = (late >= 0) & (late < valid)
        return jnp.maximum(best, jnp.max(jnp.where(inside, power, 0.0), 0))

    best = lax.fori_loop(
        0, groups, second_stage, jnp.zeros((SUB, width), jnp.float32), unroll=4
    )
    norm = jnp.sum(norm, 0, keepdims=True) * (SCALE * SCALE)
    out_ref[0] = jnp.max(best, 0, keepdims=True) / norm


def correlate(received, strain, starts, rows):
    parts, _, depth2, _ = received.shape
    segs = strain.shape[3]
    bins = parts * RADIX * depth2 // 2
    base, turn, second = tables(bins)
    per_tile = LANES // segs
    tiles = -(-rows // per_tile)
    width = 2 * LANES if tiles % 2 == 0 else LANES
    steps = tiles * LANES // width
    starts = jnp.tile(jnp.repeat(starts, per_tile), width // LANES)
    starts = jnp.broadcast_to(starts[None, :], (SUB, width))
    groups = 2 * bins // RADIX // SUB
    whole = pl.BlockSpec(memory_space=pltpu.VMEM)
    out = pl.pallas_call(
        functools.partial(kernel, bins),
        grid=(steps,),
        out_shape=jax.ShapeDtypeStruct((steps, 1, width), jnp.float32),
        in_specs=[whole] * 6,
        out_specs=pl.BlockSpec((1, 1, width), lambda i: (i, 0, 0)),
        scratch_shapes=[
            pltpu.VMEM(base.shape, jnp.float32),
            pltpu.VMEM((RADIX, groups * 2 * SUB, 2 * bins // RADIX), jnp.bfloat16),
            pltpu.VMEM((RADIX, parts * depth2, LANES), jnp.float32),
            pltpu.VMEM((groups, RADIX, 2 * SUB, width), jnp.bfloat16),
        ],
        compiler_params=pltpu.CompilerParams(vmem_limit_bytes=50 * 1024 * 1024),
    )(received, strain, jnp.asarray(base), jnp.asarray(turn), jnp.asarray(second), starts)
    out = out.reshape(tiles, segs, per_tile)
    return out.transpose(0, 2, 1).reshape(tiles * per_tile, segs)[:rows]


def join_parts(pieces, depth):
    if depth % SUB == 0:
        return pieces
    parts, _, _, last = pieces.shape
    pieces = pieces.reshape(parts, RADIX, 2, depth, last).transpose(1, 2, 0, 3, 4)
    return pieces.reshape(1, RADIX, 2 * parts * depth, last)


def share(piece, axes):
    count = lax.axis_size(axes)
    return lax.all_to_all(jnp.broadcast_to(piece[None], (count,) + piece.shape), axes, 0, 0, tiled=True)


def on_device(spectra, templates, valid_start):
    parts = lax.axis_size("freq")
    bins_here, _, rows_here = templates.shape
    depth = bins_here // RADIX
    rows = rows_here // parts
    bank = templates.reshape(depth, RADIX, 2, parts, rows).transpose(3, 1, 2, 0, 4)
    strain = share(spectra.reshape(bins_here * 2, -1).T, "group")
    segs = strain.shape[0] * strain.shape[1]
    strain = strain.reshape(segs, depth, RADIX, 2).transpose(2, 3, 1, 0)
    strain = jnp.broadcast_to(strain[None], (parts,) + strain.shape)
    bank = jnp.concatenate([bank, strain], 4)
    bank = jnp.pad(bank, ((0, 0),) * 4 + ((0, LANES - rows - segs),))
    bank = bank.reshape(parts, RADIX, 2 * depth, LANES)
    received = lax.all_to_all(bank, "freq", 0, 0, tiled=True)
    strain = received[..., rows : rows + segs]
    peaks = correlate(join_parts(received, depth), join_parts(strain, depth), valid_start, rows)
    peaks = share(peaks.reshape(1, -1), "freq")
    return peaks.reshape(rows_here, -1)


def solution(mesh):
    in_specs = (P("freq", None, "group"), P("freq", None, "group"), P())
    out_specs = P("group", None)
    return jax.shard_map(
        on_device, mesh=mesh, in_specs=in_specs, out_specs=out_specs, check_vma=False
    )
```

profile of v0, /device:TPU:0, one launch (start us, length us, event | category | flops | bytes accessed | tf_op | source)
XLA Modules:
  0.0 97.7 jit_solution(6799632850957194110)
XLA Ops:
  0.0 0.9 copy.15
  0.9 0.1 copy.16
  1.0 0.6 broadcast_in_dim.14
  1.6 4.3 %all-to-all-start = ((bf16[4,4,512]{2,1,0:T(4,128)(2,1)}), bf16[4,4,512]{2,1,0:T(4,128)(2,1)S(1)}, u32[]{:S(2)}, u32[]{:S(2)}) async-start(bf16[4,4,512]{2,1,0:T(4,128)(2,1)} %broadcast_in_dim.14), calls=%async_computation | async-start | bytes 32768 | tf_op jit(solution)/shard_map/all_to_all | solution.py:164
  5.9 2.8 %reshape.25 = bf16[16,16,2,8,80]{4,3,2,1,0:T(8,128)(2,1)S(1)} reshape(bf16[256,2,640]{2,1,0:T(2,128)(2,1)} %param.7) | data formatting | bytes 1310720 | tf_op jit(solution)/shard_map/reshape | solution.py:172
  8.6 0.7 copy.22
  9.3 0.4 all-to-all-done
  9.7 0.3 copy.17
  10.1 0.3 reshape.27
  10.4 0.1 copy.18
  10.4 0.2 broadcast_in_dim.30
  10.6 1.7 %fusion.2 = bf16[8,16,2,16,128]{4,3,2,1,0:T(8,128)(2,1)} fusion(bf16[8,16,2,16,16]{4,3,2,1,0:T(8,128)(2,1)S(1)} %broadcast_in_dim.30, bf16[8,16,2,16,80]{4,3,2,1,0:T(8,128)(2,1)S(1)} %bitcast.13), kind=kLoop, calls=%fused_computation.3 | loop fusion | flops 3670016 | bytes 1835008 | tf_op jit(solution)/shard_map/concatenate | solution.py:177
  12.3 6.4 %all-to-all-start.1 = ((bf16[8,16,32,128]{3,2,1,0:T(8,128)(2,1)}), bf16[8,16,32,128]{3,2,1,0:T(8,128)(2,1)S(1)}, u32[]{:S(2)}, u32[]{:S(2)}) async-start(bf16[8,16,32,128]{3,2,1,0:T(8,128)(2,1)} %bitcast.4), calls=%async_computation.1 | async-start | bytes 2097152 | tf_op jit(solution)/shard_map/all_to_all | solution.py:180
  18.7 0.0 copy-done.3
  18.7 0.1 broadcast_in_dim.31
  18.8 0.1 tile.7
  18.9 0.0 copy-start
  18.9 0.0 copy-start.1
  18.9 0.0 copy-start.2
  18.9 25.8 %all-to-all-done.1.r_ref = bf16[8,16,32,128]{3,2,1,0:T(8,128)(2,1)S(1)} async-done(((bf16[8,16,32,128]{3,2,1,0:T(8,128)(2,1)}), bf16[8,16,32,128]{3,2,1,0:T(8,128)(2,1)S(1)}, u32[]{:S(2)}, u32[]{:S(2)}) %all-to-all-start.1) | async-done | bytes 1048608 | tf_op jit(solution)/shard_map/all_to_all | solution.py:180
  44.7 0.4 slice.4.d_ref
  45.1 0.0 copy-done
  45.1 0.0 copy-done.1
  45.1 0.0 copy-done.2
  45.1 41.0 %shard_map.64 = f32[5,1,256]{2,1,0:T(1,128)S(1)} custom-call(bf16[8,16,32,128]{3,2,1,0:T(8,128)(2,1)S(1)} %all-to-all-done.1.r_ref, bf16[8,16,32,16]{3,2,1,0:T(8,128)(2,1)S(1)} %slice.4.d_ref, f32[32,2,8,256]{3,2,1,0:T(8,128)S(1)} %copy-done, f32[2,32,8,1]{3,2,1,0:T(8,128)S(1)} %copy-done.1, bf16[256,256]{1,0:T(8,128)(2,1)S(1)} %copy-done.2, ...), custom_call_target="tpu_custom_call" | custom-call | tf_op jit(solution)/shard_map/pallas_call | solution.py:136
  86.2 0.1 reshape.29
  86.3 0.1 copy.19
  86.3 0.1 broadcast_in_dim.34
  86.5 10.2 %all_to_all.15 = f32[8,1,1280]{2,1,0:T(1,128)S(1)} all-to-all(f32[8,1,1280]{2,1,0:T(1,128)S(1)} %broadcast_in_dim.35), channel_id=1, replica_groups=mesh['group'=4,'freq'=8] {'freq'}, dimensions={0} | all-to-all | bytes 81920 | tf_op jit(solution)/shard_map/all_to_all | solution.py:164
  96.6 0.1 reduce.1
  96.7 0.1 reshape.30
  96.9 0.8 copy.20
  (5 shorter events, 0.1 us)
Async XLA Ops:
  1.6 8.1 %all-to-all-start = ((bf16[4,4,512]{2,1,0:T(4,128)(2,1)}), bf16[4,4,512]{2,1,0:T(4,128)(2,1)S(1)}, u32[]{:S(2)}, u32[]{:S(2)}) async-start(bf16[4,4,512]{2,1,0:T(4,128)(2,1)} %broadcast_in_dim.14), calls=%async_computation | async-start | bytes 32768 | tf_op jit(solution)/shard_map/all_to_all | solution.py:164
  12.3 6.4 %copy-start.3 = (s32[16]{0:T(128)S(1)}, s32[16]{0:T(128)}, u32[]{:S(2)}) copy-start(s32[16]{0:T(128)} %param.8) | copy-start | bytes 196
  12.3 32.4 %all-to-all-start.1 = ((bf16[8,16,32,128]{3,2,1,0:T(8,128)(2,1)}), bf16[8,16,32,128]{3,2,1,0:T(8,128)(2,1)S(1)}, u32[]{:S(2)}, u32[]{:S(2)}) async-start(bf16[8,16,32,128]{3,2,1,0:T(8,128)(2,1)} %bitcast.4), calls=%async_computation.1 | async-start | bytes 2097152 | tf_op jit(solution)/shard_map/all_to_all | solution.py:180
  18.9 26.2 %copy-start = (f32[32,2,8,256]{3,2,1,0:T(8,128)S(1)}, f32[32,2,8,256]{3,2,1,0:T(8,128)}, u32[]{:S(2)}) copy-start(f32[32,2,8,256]{3,2,1,0:T(8,128)} %constant.9.clone.base_ref) | copy-start | bytes 1572868
  18.9 26.2 %copy-start.1 = (f32[2,32,8,1]{3,2,1,0:T(8,128)S(1)}, f32[2,32,8,1]{3,2,1,0:T(8,128)}, u32[]{:S(2)}) copy-start(f32[2,32,8,1]{3,2,1,0:T(8,128)} %constant.10.clone.turn_ref) | copy-start | bytes 6148
  18.9 26.2 %copy-start.2 = (bf16[256,256]{1,0:T(8,128)(2,1)S(1)}, bf16[256,256]{1,0:T(8,128)(2,1)}, u32[]{:S(2)}) copy-start(bf16[256,256]{1,0:T(8,128)(2,1)} %constant.11.clone.w2_ref) | copy-start | bytes 393220
where the time goes:
time: 98 us; the launch traced here: 97.7 us
  Pallas kernels  41 us (42%)
  waiting for transfers between devices  26.2 us (27%)
  starting transfers between devices  10.6 us (11%)
  blocking collectives  10.2 us (10%)
  local copies, waits for them, and re-layouts  7.61 us (8%)
  other arithmetic  1.82 us (2%)
    pallas_call x1, Pallas kernels, correlate(): pl.pallas_call(functools.partial(kernel, bins), grid=(steps,), out_shape=...  41 us
    all_to_all x1, waiting for transfers between devices, on_device(): received = lax.all_to_all(bank, 'freq', 0, 0, tiled=True)  25.8 us
    all_to_all x1, blocking collectives, share(): lax.all_to_all(jnp.broadcast_to(piece[None], (count,) + piece.shape), axe...  10.2 us
    all_to_all x1, starting transfers between devices, on_device(): received = lax.all_to_all(bank, 'freq', 0, 0, tiled=True)  6.37 us
    all_to_all x1, starting transfers between devices, share(): lax.all_to_all(jnp.broadcast_to(piece[None], (count,) + piece.shape), axe...  4.26 us
    reshape x2, local copies, waits for them, and re-layouts, on_device(): templates.reshape(depth, RADIX, 2, parts, rows).transpose(3, 1, 2, 0, 4)  3.44 us
  transfers between devices with their start and end apart: 2, of which 2 were waited for; matrix products, arithmetic and copies ran while one was open for 4% of the time, Pallas kernels for 0%

commit v1 on v0

--- a/solution.py
+++ b/solution.py
@@ -184,9 +184,325 @@
     return peaks.reshape(rows_here, -1)
 
 
+MESH = pl.DeviceIdType.MESH
+
+
+def fused_tables(bins):
+    base, turn, _ = tables(bins)
+    groups, _, _, cols = base.shape
+    base = base.reshape(groups, 2, SUB, 2, cols // (2 * SUB), SUB)
+    base = base.transpose(0, 1, 2, 4, 3, 5).reshape(groups, 2, SUB, cols)
+    b = np.arange(RADIX)
+    angle = 2.0 * math.pi * ((b[: RADIX // 2, None] * b[None, :]) % RADIX) / RADIX
+    second = rotation(angle, 0, 2) * SCALE
+    second = np.kron(second.reshape(RADIX, 2 * RADIX), np.eye(SUB))
+    return base, turn, second.astype(jnp.bfloat16)
+
+
+def block_transpose(rows, size):
+    count = len(rows)
+    lane = lax.broadcasted_iota(jnp.int32, rows[0].shape, rows[0].ndim - 1) // size
+    step = count // 2
+    while step:
+        low = (lane // step) % 2 == 0
+        fresh = list(rows)
+        for i in range(count):
+            if i & step == 0:
+                first, second = rows[i], rows[i + step]
+                axis = first.ndim - 1
+                fresh[i] = jnp.where(low, first, pltpu.roll(second, size * step, axis))
+                fresh[i + step] = jnp.where(low, pltpu.roll(first, LANES - size * step, axis), second)
+        rows = fresh
+        step //= 2
+    return rows
+
+
+def fused_kernel(
+    x_hbm, s_ref, vs_ref, base_hbm, turn_hbm, w2_hbm, out_ref,
+    x_ref, send_ref, recv_ref, work_ref, turn_ref, w2_ref, w1_ref, strain_ref, dexp_ref, y_ref, peak_ref,
+    load_sem, table_sem, send_sem, recv_sem, ssend_sem, srecv_sem, gsend_sem, grecv_sem, psend_sem, precv_sem,
+):
+    tiles, parts = recv_ref.shape[:2]
+    halves, highs = recv_ref.shape[2:4]
+    lows = RADIX // highs
+    size = LANES // parts
+    segs = vs_ref.shape[0]
+    width = y_ref.shape[3]
+    groups = y_ref.shape[0]
+    crowd = strain_ref.shape[0]
+    bins_here = x_ref.shape[1]
+    rows = 2 * SUB * RADIX
+    lags = 2 * parts * bins_here
+    me = lax.axis_index("freq")
+    team = lax.axis_index("group")
+
+    def load(tile):
+        return pltpu.make_async_copy(
+            x_hbm.at[:, :, pl.ds(tile * LANES, LANES)], x_ref.at[tile], load_sem.at[tile]
+        )
+
+    table_copies = [
+        pltpu.make_async_copy(base_hbm, work_ref, table_sem.at[0]),
+        pltpu.make_async_copy(turn_hbm, turn_ref, table_sem.at[1]),
+        pltpu.make_async_copy(w2_hbm, w2_ref, table_sem.at[2]),
+    ]
+    for tile in range(tiles):
+        load(tile).start()
+    for copy in table_copies:
+        copy.start()
+
+    barrier = pltpu.get_barrier_semaphore()
+    for hop in range(1, parts):
+        pl.semaphore_signal(
+            barrier, inc=1, device_id={"freq": lax.rem(me + hop, parts)}, device_id_type=MESH
+        )
+    for hop in range(1, crowd):
+        pl.semaphore_signal(
+            barrier, inc=1, device_id={"group": lax.rem(team + hop, crowd)}, device_id_type=MESH
+        )
+    pl.semaphore_wait(barrier, parts + crowd - 2)
+
+    def strain_copy(source, target):
+        return pltpu.make_async_remote_copy(
+            src_ref=s_ref, dst_ref=strain_ref.at[team, source],
+            send_sem=ssend_sem.at[target], recv_sem=srecv_sem.at[source],
+            device_id={"freq": target}, device_id_type=MESH,
+        )
+
+    def team_copy(source, target):
+        return pltpu.make_async_remote_copy(
+            src_ref=strain_ref.at[team], dst_ref=strain_ref.at[source],
+            send_sem=gsend_sem.at[target], recv_sem=grecv_sem.at[source],
+            device_id={"group": target}, device_id_type=MESH,
+        )
+
+    def bank_copy(tile, source, target):
+        return pltpu.make_async_remote_copy(
+            src_ref=send_ref.at[tile, target], dst_ref=recv_ref.at[tile, source],
+            send_sem=send_sem.at[tile, target], recv_sem=recv_sem.at[tile, source],
+            device_id={"freq": target}, device_id_type=MESH,
+        )
+
+    def peak_copy(source, target):
+        return pltpu.make_async_remote_copy(
+            src_ref=peak_ref.at[me], dst_ref=peak_ref.at[source],
+            send_sem=psend_sem.at[target], recv_sem=precv_sem.at[source],
+            device_id={"freq": target}, device_id_type=MESH,
+        )
+
+    def others(count, here):
+        return [lax.rem(here + hop, count) for hop in range(1, count)]
+
+    for target in others(parts, me):
+        strain_copy(me, target).start()
+    strain_ref[team, me] = s_ref[...]
+
+    place = lax.broadcasted_iota(jnp.int32, (rows, rows), 0)
+    origin = ((place % SUB) * RADIX + place // (2 * SUB)) * 2 + (place // SUB) % 2
+    sort = (lax.broadcasted_iota(jnp.int32, (rows, rows), 1) == origin).astype(jnp.bfloat16)
+
+    def prepare(tile):
+        load(tile).wait()
+        x = x_ref[tile].reshape(halves, rows, LANES)
+        x = jnp.stack([jnp.dot(sort, x[h], preferred_element_type=jnp.float32) for h in range(halves)])
+        x = x.reshape(halves * highs, lows, 2 * SUB, LANES)
+        x = block_transpose([x[:, i] for i in range(lows)], size)
+        for p in range(parts):
+            send_ref[tile, p] = x[p].astype(jnp.bfloat16).reshape(halves, highs, 2 * SUB, LANES)
+        for target in others(parts, me):
+            bank_copy(tile, me, target).start()
+        recv_ref[tile, me] = send_ref[tile, me]
+
+    for tile in range(tiles):
+        prepare(tile)
+        if tile == min(1, tiles - 1):
+            for source in others(parts, me):
+                strain_copy(source, source).wait_recv()
+            for target in others(crowd, team):
+                team_copy(team, target).start()
+
+    for copy in table_copies:
+        copy.wait()
+
+    @pl.loop(0, RADIX)
+    def _(b):
+        w1_ref[b] = work_ref[...].reshape(w1_ref.shape[1:]).astype(jnp.bfloat16)
+        top, bottom = work_ref[:, 0], work_ref[:, 1]
+        cosine, sine = turn_ref[0], turn_ref[1]
+        work_ref[:, 0] = top * cosine - bottom * sine
+        work_ref[:, 1] = bottom * cosine + top * sine
+
+    for source in others(crowd, team):
+        team_copy(source, source).wait_recv()
+
+    spread = (
+        lax.broadcasted_iota(jnp.int32, (segs, LANES), 0)
+        == lax.broadcasted_iota(jnp.int32, (segs, LANES), 1) % segs
+    ).astype(jnp.bfloat16)
+    for f in range(parts):
+        piece = jnp.concatenate([strain_ref[g, f] for g in range(crowd)], 0)
+        piece = lax.dot_general(
+            piece, spread, (((0,), (0,)), ((), ())), preferred_element_type=jnp.float32
+        )
+        piece = piece.reshape(halves, RADIX, 2 * SUB, LANES)
+        for h in range(halves):
+            dexp_ref[:, f * halves + h] = piece[h]
+
+    seg = lax.broadcasted_iota(jnp.int32, (SUB, LANES), 1) % segs
+    shift = jnp.zeros((SUB, LANES), jnp.int32)
+    for s in range(segs):
+        shift = jnp.where(seg == s, vs_ref[s], shift)
+    a = lax.broadcasted_iota(jnp.int32, (parts * halves, SUB, LANES), 0) * SUB
+    a = a + lax.broadcasted_iota(jnp.int32, (parts * halves, SUB, LANES), 1)
+    unit = 2.0 * math.pi / lags
+    phase = ((a * shift[None] * RADIX + lags // 2) % lags - lags // 2).astype(jnp.float32) * unit
+    step_phase = shift.astype(jnp.float32) * unit
+    step_cos, step_sin = jnp.cos(step_phase)[None], jnp.sin(step_phase)[None]
+
+    def rotate(b, carry):
+        cosine, sine = carry
+        d0, d1 = dexp_ref[b, :, :SUB], dexp_ref[b, :, SUB:]
+        dexp_ref[b, :, :SUB] = d0 * cosine - d1 * sine
+        dexp_ref[b, :, SUB:] = d0 * sine + d1 * cosine
+        return cosine * step_cos - sine * step_sin, cosine * step_sin + sine * step_cos
+
+    lax.fori_loop(0, RADIX, rotate, (jnp.cos(phase), jnp.sin(phase)))
+
+    blocks = parts * halves
+    lane_template = lax.broadcasted_iota(jnp.int32, (LANES, width), 1) // segs
+    bank_row = lax.broadcasted_iota(jnp.int32, (LANES, width), 0)
+    collect = (bank_row % size == lane_template).astype(jnp.float32)
+
+    @pl.loop(0, tiles)
+    def _(tile):
+        for source in others(parts, me):
+            bank_copy(tile, source, source).wait_recv()
+
+        def first_stage(i, norm):
+            pick = (bank_row == i * size + lane_template).astype(jnp.bfloat16)
+            for high in range(highs):
+                b = high * lows + i
+                piece = recv_ref[tile, :, :, high].reshape(blocks * 2 * SUB, LANES)
+                bank = jnp.dot(piece, pick, preferred_element_type=jnp.float32)
+                bank = bank.reshape(blocks, 2 * SUB, width)
+                h0, h1 = bank[:, :SUB], bank[:, SUB:]
+                d0, d1 = dexp_ref[b, :, :SUB], dexp_ref[b, :, SUB:]
+                d0 = jnp.concatenate([d0] * (width // LANES), 2)
+                d1 = jnp.concatenate([d1] * (width // LANES), 2)
+                cross = jnp.concatenate([h0 * d0 + h1 * d1, h0 * d1 - h1 * d0], 1)
+                cross = cross.reshape(blocks * 2 * SUB, width).astype(jnp.bfloat16)
+                y = jnp.dot(w1_ref[b], cross, preferred_element_type=jnp.float32)
+                y_ref[:, b] = y.astype(jnp.bfloat16).reshape(groups, 2 * SUB, width)
+            return norm
+
+        lax.fori_loop(0, lows, first_stage, 0)
+
+        def add_squares(f, total):
+            piece = recv_ref[tile, f].astype(jnp.float32).reshape(-1, SUB, LANES)
+            return total + jnp.sum(piece * piece, 0)
+
+        norm = lax.fori_loop(0, parts, add_squares, jnp.zeros((SUB, LANES), jnp.float32))
+        norm = jnp.dot(norm, collect, precision=lax.Precision.HIGHEST, preferred_element_type=jnp.float32)
+        norm = jnp.sum(norm, 0, keepdims=True) * (SCALE * SCALE)
+
+        def second_stage(g, best):
+            z = jnp.dot(
+                w2_ref[...], y_ref[g].reshape(w2_ref.shape[1], width), preferred_element_type=jnp.float32
+            )
+            half = z.shape[0] // 2
+            re, im = z[:half], z[half:]
+            power = (re * re + im * im).reshape(half // SUB, SUB, width)
+            return jnp.maximum(best, jnp.max(power, 0))
+
+        best = lax.fori_loop(
+            0, groups, second_stage, jnp.zeros((SUB, width), jnp.float32), unroll=4
+        )
+        peak_ref[me, tile] = jnp.max(best, 0, keepdims=True) / norm
+
+    for target in others(parts, me):
+        peak_copy(me, target).start()
+    for source in others(parts, me):
+        peak_copy(source, source).wait_recv()
+    out_ref[...] = peak_ref[...].reshape(out_ref.shape)
+    for target in others(parts, me):
+        peak_copy(me, target).wait_send()
+        strain_copy(me, target).wait_send()
+        for tile in range(tiles):
+            bank_copy(tile, me, target).wait_send()
+    for target in others(crowd, team):
+        team_copy(team, target).wait_send()
+
+
+def fused(spectra, templates, valid_start):
+    parts, crowd = lax.axis_size("freq"), lax.axis_size("group")
+    bins_here, _, rows_here = templates.shape
+    segs_here = spectra.shape[2]
+    segs = segs_here * crowd
+    bins = bins_here * parts
+    tiles = rows_here // LANES
+    halves = bins_here // (SUB * RADIX)
+    highs = RADIX // parts
+    width = LANES // parts * segs
+    base, turn, second = fused_tables(bins)
+    strain = spectra.reshape(halves, SUB, RADIX, 2, segs_here).transpose(4, 0, 2, 3, 1)
+    strain = strain.reshape(segs_here, 2 * bins_here)
+    groups = 2 * bins // RADIX // SUB
+    anywhere = pl.BlockSpec(memory_space=pl.ANY)
+    whole = pl.BlockSpec(memory_space=pltpu.VMEM)
+    dma = pltpu.SemaphoreType.DMA
+    chunk = (halves, highs, 2 * SUB, LANES)
+    out = pl.pallas_call(
+        fused_kernel,
+        out_shape=jax.ShapeDtypeStruct((parts, tiles, width), jnp.float32),
+        in_specs=[anywhere, whole, pl.BlockSpec(memory_space=pltpu.SMEM), anywhere, anywhere, anywhere],
+        out_specs=whole,
+        scratch_shapes=[
+            pltpu.VMEM((tiles, bins_here, 2, LANES), jnp.bfloat16),
+            pltpu.VMEM((tiles, parts) + chunk, jnp.bfloat16),
+            pltpu.VMEM((tiles, parts) + chunk, jnp.bfloat16),
+            pltpu.VMEM(base.shape, jnp.float32),
+            pltpu.VMEM(turn.shape, jnp.float32),
+            pltpu.VMEM(second.shape, jnp.bfloat16),
+            pltpu.VMEM((RADIX, groups * 2 * SUB, 2 * bins // RADIX), jnp.bfloat16),
+            pltpu.VMEM((crowd, parts, segs_here, 2 * bins_here), jnp.bfloat16),
+            pltpu.VMEM((RADIX, parts * halves, 2 * SUB, LANES), jnp.float32),
+            pltpu.VMEM((groups, RADIX, 2 * SUB, width), jnp.bfloat16),
+            pltpu.VMEM((parts, tiles, 1, width), jnp.float32),
+            dma((tiles,)), dma((3,)),
+            dma((tiles, parts)), dma((tiles, parts)),
+            dma((parts,)), dma((parts,)),
+            dma((crowd,)), dma((crowd,)),
+            dma((parts,)), dma((parts,)),
+        ],
+        compiler_params=pltpu.CompilerParams(
+            vmem_limit_bytes=50 * 1024 * 1024, collective_id=0, has_side_effects=True
+        ),
+    )(templates, strain, valid_start, jnp.asarray(base), jnp.asarray(turn), jnp.asarray(second))
+    return out.transpose(1, 0, 2).reshape(rows_here, segs)
+
+
+def fits(spectra, templates):
+    parts = lax.axis_size("freq")
+    segs = spectra.shape[2] * lax.axis_size("group")
+    bins_here, _, rows_here = templates.shape
+    return (
+        parts > 1
+        and RADIX % parts == 0
+        and rows_here % LANES == 0
+        and bins_here % (SUB * RADIX) == 0
+        and LANES // parts * segs == 2 * LANES
+    )
+
+
+def dispatch(spectra, templates, valid_start):
+    if fits(spectra, templates):
+        return fused(spectra, templates, valid_start)
+    return on_device(spectra, templates, valid_start)
+
+
 def solution(mesh):
     in_specs = (P("freq", None, "group"), P("freq", None, "group"), P())
     out_specs = P("group", None)
     return jax.shard_map(
-        on_device, mesh=mesh, in_specs=in_specs, out_specs=out_specs, check_vma=False
+        dispatch, mesh=mesh, in_specs=in_specs, out_specs=out_specs, check_vma=False
     )

time: 98 us -> 58.5 us (0.60)
  waiting for transfers between devices: 26.2 us -> 0 us
  Pallas kernels: 41 us -> 52.5 us
  starting transfers between devices: 10.6 us -> 0 us
  blocking collectives: 10.2 us -> 0 us
  local copies, waits for them, and re-layouts: 7.61 us -> 5.58 us
  other arithmetic: 1.82 us -> 0 us
    all_to_all x2 -> x0, waiting for transfers between devices: 26.2 us -> none  [the longest x1 25.8 us: on_device(): received = lax.all_to_all(bank, 'freq', 0, 0, tiled=True)]
    pallas_call x1, Pallas kernels: 41 us -> 52.5 us  [fused(): pl.pallas_call(fused_kernel, out_shape=jax.ShapeDtypeStruct((parts, tiles...]
    all_to_all x2 -> x0, starting transfers between devices: 10.6 us -> none  [the longest x1 6.37 us: on_device(): received = lax.all_to_all(bank, 'freq', 0, 0, tiled=True)]
    all_to_all x1 -> x0, blocking collectives: 10.2 us -> none  [share(): lax.all_to_all(jnp.broadcast_to(piece[None], (count,) + piece.shape), axe...]
    reshape x6 -> x5, local copies, waits for them, and re-layouts: 4.72 us -> 1.89 us  [the longest x2 0.89 us: fused(): return out.transpose(1, 0, 2).reshape(rows_here, segs)]
    unnamed x9 -> x10, local copies, waits for them, and re-layouts: 0.88 us -> 3.67 us
    concatenate x1 -> x0, other arithmetic: 1.7 us -> none  [on_device(): bank = jnp.concatenate([bank, strain], 4)]
    broadcast_in_dim x7 -> x0, local copies, waits for them, and re-layouts: 0.99 us -> none  [the longest x3 0.75 us: share(): jnp.broadcast_to(piece[None], (count,) + piece.shape)]
  transfers between devices with their start and end apart: 2 -> 0, of which waited for: 2 -> 0; matrix products, arithmetic and copies ran while one was open for 4% -> 0% of each run, Pallas kernels for 0% -> 0%
where the time goes in v1:
time: 58.5 us; the launch traced here: 58.2 us
  Pallas kernels  52.5 us (90%)
  local copies, waits for them, and re-layouts  5.58 us (10%)
    pallas_call x1, Pallas kernels, fused(): pl.pallas_call(fused_kernel, out_shape=jax.ShapeDtypeStruct((parts, tiles...  52.5 us
    unnamed x10, local copies, waits for them, and re-layouts  3.67 us

profile of v1, /device:TPU:0, one launch (start us, length us, event | category | flops | bytes accessed | tf_op | source)
XLA Modules:
  0.0 58.2 jit_solution(2251461791254034173)
XLA Ops:
  0.0 0.8 %reshape.9 = bf16[2,8,16,2,4]{2,1,0,4,3:T(8,128)(2,1)S(1)} reshape(bf16[256,2,4]{0,2,1:T(4,128)(2,1)} %param.6) | data formatting | bytes 8192 | tf_op jit(solution)/shard_map/reshape | solution.py:447
  0.8 0.0 copy-start.3
  0.8 0.1 copy.8
  0.9 0.0 copy-start.4
  0.9 0.1 reshape.10.s_ref
  1.0 0.6 %copy-done.3 = bf16[128,256]{1,0:T(8,128)(2,1)S(1)} copy-done((bf16[128,256]{1,0:T(8,128)(2,1)S(1)}, bf16[128,256]{1,0:T(8,128)(2,1)}, u32[]{:S(2)}) %copy-start.3) | copy-done | bytes 65560
  1.6 0.0 copy-done.4
  1.6 0.0 copy-start
  1.6 1.1 %copy-done = bf16[256,2,640]{2,1,0:T(2,128)(2,1)S(1)} copy-done((bf16[256,2,640]{2,1,0:T(2,128)(2,1)S(1)}, bf16[256,2,640]{2,1,0:T(2,128)(2,1)}, u32[]{:S(2)}) %copy-start) | copy-done | bytes 655384
  2.7 0.0 copy-start.1
  2.7 1.0 %copy-done.1 = f32[32,2,8,256]{3,2,1,0:T(8,128)S(1)} copy-done((f32[32,2,8,256]{3,2,1,0:T(8,128)S(1)}, f32[32,2,8,256]{3,2,1,0:T(8,128)}, u32[]{:S(2)}) %copy-start.1) | copy-done | bytes 524312
  3.8 0.0 copy-start.2
  3.8 0.9 %copy-done.2 = f32[2,32,8,1]{3,2,1,0:T(8,128)S(1)} copy-done((f32[2,32,8,1]{3,2,1,0:T(8,128)S(1)}, f32[2,32,8,1]{3,2,1,0:T(8,128)}, u32[]{:S(2)}) %copy-start.2) | copy-done | bytes 2072
  4.7 52.5 %shard_map.64 = f32[8,5,256]{2,1,0:T(8,128)S(1)} custom-call(bf16[256,2,640]{2,1,0:T(2,128)(2,1)S(1)} %copy-done, bf16[4,512]{1,0:T(4,128)(2,1)S(1)} %reshape.10.s_ref, s32[16]{0:T(128)S(1)} %copy-done.4, f32[32,2,8,256]{3,2,1,0:T(8,128)S(1)} %copy-done.1, f32[2,32,8,1]{3,2,1,0:T(8,128)S(1)} %copy-done.2, bf16[128,256]{1,0:T(8,128)(2,1)S(1)} %copy-done.3), custom_call_target="tpu_custom_call" | custom-call | tf_op jit(solution)/shard_map/pallas_call | solution.py:454
  57.3 0.1 reshape.11
  57.4 0.8 %copy.10 = f32[640,16]{0,1:T(8,128)} copy(f32[640,16]{1,0:T(8,128)S(1)} %reshape.11) | data formatting | bytes 81920 | tf_op jit(solution)/shard_map/reshape | solution.py:481
  (1 shorter events, 0.0 us)
Async XLA Ops:
  0.8 0.8 %copy-start.3 = (bf16[128,256]{1,0:T(8,128)(2,1)S(1)}, bf16[128,256]{1,0:T(8,128)(2,1)}, u32[]{:S(2)}) copy-start(bf16[128,256]{1,0:T(8,128)(2,1)} %constant.8.clone.w2_hbm) | copy-start | bytes 196612
  0.9 0.7 %copy-start.4 = (s32[16]{0:T(128)S(1)}, s32[16]{0:T(128)}, u32[]{:S(2)}) copy-start(s32[16]{0:T(128)} %vs_ref.1) | copy-start | bytes 196
  1.6 1.1 %copy-start = (bf16[256,2,640]{2,1,0:T(2,128)(2,1)S(1)}, bf16[256,2,640]{2,1,0:T(2,128)(2,1)}, u32[]{:S(2)}) copy-start(bf16[256,2,640]{2,1,0:T(2,128)(2,1)} %x_hbm.1) | copy-start | bytes 1966084
  2.7 1.0 %copy-start.1 = (f32[32,2,8,256]{3,2,1,0:T(8,128)S(1)}, f32[32,2,8,256]{3,2,1,0:T(8,128)}, u32[]{:S(2)}) copy-start(f32[32,2,8,256]{3,2,1,0:T(8,128)} %constant.6.clone.base_hbm) | copy-start | bytes 1572868
  3.8 0.9 %copy-start.2 = (f32[2,32,8,1]{3,2,1,0:T(8,128)S(1)}, f32[2,32,8,1]{3,2,1,0:T(8,128)}, u32[]{:S(2)}) copy-start(f32[2,32,8,1]{3,2,1,0:T(8,128)} %constant.7.clone.turn_hbm) | copy-start | bytes 6148

commit v2 on v1

--- a/solution.py
+++ b/solution.py
@@ -193,9 +193,9 @@
     base = base.reshape(groups, 2, SUB, 2, cols // (2 * SUB), SUB)
     base = base.transpose(0, 1, 2, 4, 3, 5).reshape(groups, 2, SUB, cols)
     b = np.arange(RADIX)
-    angle = 2.0 * math.pi * ((b[: RADIX // 2, None] * b[None, :]) % RADIX) / RADIX
+    angle = 2.0 * math.pi * ((b[: RADIX * 3 // 4, None] * b[None, :]) % RADIX) / RADIX
     second = rotation(angle, 0, 2) * SCALE
-    second = np.kron(second.reshape(RADIX, 2 * RADIX), np.eye(SUB))
+    second = np.kron(second.reshape(-1, 2 * RADIX), np.eye(SUB))
     return base, turn, second.astype(jnp.bfloat16)
 
 
@@ -218,8 +218,9 @@
 
 
 def fused_kernel(
-    x_hbm, s_ref, vs_ref, base_hbm, turn_hbm, w2_hbm, out_ref,
-    x_ref, send_ref, recv_ref, work_ref, turn_ref, w2_ref, w1_ref, strain_ref, dexp_ref, y_ref, peak_ref,
+    x_hbm, s_hbm, vs_ref, base_hbm, turn_hbm, w2_hbm, out_ref,
+    x_ref, own_ref, send_ref, recv_ref, work_ref, turn_ref, w2_ref, w1_ref, s_ref, strain_ref, dexp_ref,
+    cross_ref, y_ref, peak_ref,
     load_sem, table_sem, send_sem, recv_sem, ssend_sem, srecv_sem, gsend_sem, grecv_sem, psend_sem, precv_sem,
 ):
     tiles, parts = recv_ref.shape[:2]
@@ -233,8 +234,14 @@
     bins_here = x_ref.shape[1]
     rows = 2 * SUB * RADIX
     lags = 2 * parts * bins_here
+    inner = lags // RADIX
+    quarter = lags // 4
+    blocks = parts * halves
     me = lax.axis_index("freq")
     team = lax.axis_index("group")
+
+    def others(count, here):
+        return [lax.rem(here + hop, count) for hop in range(1, count)]
 
     def load(tile):
         return pltpu.make_async_copy(
@@ -242,25 +249,22 @@
         )
 
     table_copies = [
-        pltpu.make_async_copy(base_hbm, work_ref, table_sem.at[0]),
-        pltpu.make_async_copy(turn_hbm, turn_ref, table_sem.at[1]),
-        pltpu.make_async_copy(w2_hbm, w2_ref, table_sem.at[2]),
+        pltpu.make_async_copy(s_hbm, own_ref, table_sem.at[0]),
+        pltpu.make_async_copy(base_hbm, work_ref, table_sem.at[1]),
+        pltpu.make_async_copy(turn_hbm, turn_ref, table_sem.at[2]),
+        pltpu.make_async_copy(w2_hbm, w2_ref, table_sem.at[3]),
     ]
+    table_copies[0].start()
     for tile in range(tiles):
         load(tile).start()
-    for copy in table_copies:
+    for copy in table_copies[1:]:
         copy.start()
 
     barrier = pltpu.get_barrier_semaphore()
-    for hop in range(1, parts):
-        pl.semaphore_signal(
-            barrier, inc=1, device_id={"freq": lax.rem(me + hop, parts)}, device_id_type=MESH
-        )
-    for hop in range(1, crowd):
-        pl.semaphore_signal(
-            barrier, inc=1, device_id={"group": lax.rem(team + hop, crowd)}, device_id_type=MESH
-        )
-    pl.semaphore_wait(barrier, parts + crowd - 2)
+    for target in others(parts, me):
+        pl.semaphore_signal(barrier, inc=1, device_id={"freq": target}, device_id_type=MESH)
+    for target in others(crowd, team):
+        pl.semaphore_signal(barrier, inc=1, device_id={"group": target}, device_id_type=MESH)
 
     def strain_copy(source, target):
         return pltpu.make_async_remote_copy(
@@ -290,38 +294,38 @@
             device_id={"freq": target}, device_id_type=MESH,
         )
 
-    def others(count, here):
-        return [lax.rem(here + hop, count) for hop in range(1, count)]
-
-    for target in others(parts, me):
-        strain_copy(me, target).start()
-    strain_ref[team, me] = s_ref[...]
-
     place = lax.broadcasted_iota(jnp.int32, (rows, rows), 0)
     origin = ((place % SUB) * RADIX + place // (2 * SUB)) * 2 + (place // SUB) % 2
     sort = (lax.broadcasted_iota(jnp.int32, (rows, rows), 1) == origin).astype(jnp.bfloat16)
 
-    def prepare(tile):
+    table_copies[0].wait()
+    for tile in range(tiles):
         load(tile).wait()
+    strain = own_ref[...].reshape(halves, rows, own_ref.shape[2])
+    strain = [
+        lax.dot_general(strain[h], sort, (((0,), (1,)), ((), ())), preferred_element_type=jnp.float32)
+        for h in range(halves)
+    ]
+    s_ref[...] = jnp.concatenate(strain, 1).astype(jnp.bfloat16)
+    for tile in range(tiles):
         x = x_ref[tile].reshape(halves, rows, LANES)
         x = jnp.stack([jnp.dot(sort, x[h], preferred_element_type=jnp.float32) for h in range(halves)])
         x = x.reshape(halves * highs, lows, 2 * SUB, LANES)
         x = block_transpose([x[:, i] for i in range(lows)], size)
         for p in range(parts):
             send_ref[tile, p] = x[p].astype(jnp.bfloat16).reshape(halves, highs, 2 * SUB, LANES)
+
+    pl.semaphore_wait(barrier, parts + crowd - 2)
+    for target in others(parts, me):
+        strain_copy(me, target).start()
+    for tile in range(tiles):
         for target in others(parts, me):
             bank_copy(tile, me, target).start()
+    strain_ref[team, me] = s_ref[...]
+    for tile in range(tiles):
         recv_ref[tile, me] = send_ref[tile, me]
 
-    for tile in range(tiles):
-        prepare(tile)
-        if tile == min(1, tiles - 1):
-            for source in others(parts, me):
-                strain_copy(source, source).wait_recv()
-            for target in others(crowd, team):
-                team_copy(team, target).start()
-
-    for copy in table_copies:
+    for copy in table_copies[1:]:
         copy.wait()
 
     @pl.loop(0, RADIX)
@@ -332,76 +336,103 @@
         work_ref[:, 0] = top * cosine - bottom * sine
         work_ref[:, 1] = bottom * cosine + top * sine
 
+    for source in others(parts, me):
+        strain_copy(source, source).wait_recv()
+    for target in others(crowd, team):
+        team_copy(team, target).start()
     for source in others(crowd, team):
         team_copy(source, source).wait_recv()
+
+    seg = lax.broadcasted_iota(jnp.int32, (SUB, LANES), 1) % segs
+    start = jnp.zeros((SUB, LANES), jnp.int32)
+    for s in range(segs):
+        start = jnp.where(seg == s, vs_ref[s], start)
+    turns = (start >= quarter).astype(jnp.int32) + (start >= 2 * quarter).astype(jnp.int32)
+    rest = start - turns * quarter
+    step_cos = 1.0 - turns.astype(jnp.float32)
+    step_sin = (turns == 1).astype(jnp.float32)
 
     spread = (
         lax.broadcasted_iota(jnp.int32, (segs, LANES), 0)
         == lax.broadcasted_iota(jnp.int32, (segs, LANES), 1) % segs
     ).astype(jnp.bfloat16)
+    unit = (jnp.ones((SUB, LANES), jnp.float32), jnp.zeros((SUB, LANES), jnp.float32))
+    factors = [unit]
+    for b in range(1, 4):
+        c, s = factors[-1]
+        factors.append((c * step_cos - s * step_sin, c * step_sin + s * step_cos))
     for f in range(parts):
         piece = jnp.concatenate([strain_ref[g, f] for g in range(crowd)], 0)
         piece = lax.dot_general(
             piece, spread, (((0,), (0,)), ((), ())), preferred_element_type=jnp.float32
         )
-        piece = piece.reshape(halves, RADIX, 2 * SUB, LANES)
+        piece = piece.reshape(halves, RADIX, 2, SUB, LANES)
         for h in range(halves):
-            dexp_ref[:, f * halves + h] = piece[h]
-
-    seg = lax.broadcasted_iota(jnp.int32, (SUB, LANES), 1) % segs
-    shift = jnp.zeros((SUB, LANES), jnp.int32)
-    for s in range(segs):
-        shift = jnp.where(seg == s, vs_ref[s], shift)
-    a = lax.broadcasted_iota(jnp.int32, (parts * halves, SUB, LANES), 0) * SUB
-    a = a + lax.broadcasted_iota(jnp.int32, (parts * halves, SUB, LANES), 1)
-    unit = 2.0 * math.pi / lags
-    phase = ((a * shift[None] * RADIX + lags // 2) % lags - lags // 2).astype(jnp.float32) * unit
-    step_phase = shift.astype(jnp.float32) * unit
-    step_cos, step_sin = jnp.cos(step_phase)[None], jnp.sin(step_phase)[None]
-
-    def rotate(b, carry):
-        cosine, sine = carry
-        d0, d1 = dexp_ref[b, :, :SUB], dexp_ref[b, :, SUB:]
-        dexp_ref[b, :, :SUB] = d0 * cosine - d1 * sine
-        dexp_ref[b, :, SUB:] = d0 * sine + d1 * cosine
-        return cosine * step_cos - sine * step_sin, cosine * step_sin + sine * step_cos
-
-    lax.fori_loop(0, RADIX, rotate, (jnp.cos(phase), jnp.sin(phase)))
-
-    blocks = parts * halves
+            for b in range(RADIX):
+                c, s = factors[b % 4]
+                d0, d1 = piece[h, b, 0], piece[h, b, 1]
+                dexp_ref[b, f * halves + h, :SUB] = d0 * c - d1 * s
+                dexp_ref[b, f * halves + h, SUB:] = d0 * s + d1 * c
+
     lane_template = lax.broadcasted_iota(jnp.int32, (LANES, width), 1) // segs
     bank_row = lax.broadcasted_iota(jnp.int32, (LANES, width), 0)
     collect = (bank_row % size == lane_template).astype(jnp.float32)
+    offset = lax.broadcasted_iota(jnp.int32, (SUB, LANES), 0) - rest
+    offset = jnp.concatenate([offset] * (width // LANES), 1)
+
+    def expand(tile, i):
+        pick = (bank_row == i * size + lane_template).astype(jnp.bfloat16)
+        for high in range(highs):
+            b = high * lows + i
+            piece = recv_ref[tile, :, :, high].reshape(blocks * 2 * SUB, LANES)
+            bank = jnp.dot(piece, pick, preferred_element_type=jnp.float32)
+            bank = bank.reshape(blocks, 2 * SUB, width)
+            h0, h1 = bank[:, :SUB], bank[:, SUB:]
+            d0, d1 = dexp_ref[b, :, :SUB], dexp_ref[b, :, SUB:]
+            d0 = jnp.concatenate([d0] * (width // LANES), 2)
+            d1 = jnp.concatenate([d1] * (width // LANES), 2)
+            cross = jnp.concatenate([h0 * d0 + h1 * d1, h0 * d1 - h1 * d0], 1)
+            cross_ref[b] = cross.reshape(blocks * 2 * SUB, width).astype(jnp.bfloat16)
+
+    def transform(i):
+        for high in range(highs):
+            b = high * lows + i
+            y = jnp.dot(w1_ref[b], cross_ref[b], preferred_element_type=jnp.float32)
+            y_ref[:, b] = y.astype(jnp.bfloat16).reshape(groups, 2 * SUB, width)
+
+    def arrive(tile):
+        for source in others(parts, me):
+            bank_copy(tile, source, source).wait_recv()
+
+    chunk = 4
+    arrive(0)
+    for i in range(chunk):
+        expand(0, i)
 
     @pl.loop(0, tiles)
     def _(tile):
-        for source in others(parts, me):
-            bank_copy(tile, source, source).wait_recv()
-
-        def first_stage(i, norm):
-            pick = (bank_row == i * size + lane_template).astype(jnp.bfloat16)
-            for high in range(highs):
-                b = high * lows + i
-                piece = recv_ref[tile, :, :, high].reshape(blocks * 2 * SUB, LANES)
-                bank = jnp.dot(piece, pick, preferred_element_type=jnp.float32)
-                bank = bank.reshape(blocks, 2 * SUB, width)
-                h0, h1 = bank[:, :SUB], bank[:, SUB:]
-                d0, d1 = dexp_ref[b, :, :SUB], dexp_ref[b, :, SUB:]
-                d0 = jnp.concatenate([d0] * (width // LANES), 2)
-                d1 = jnp.concatenate([d1] * (width // LANES), 2)
-                cross = jnp.concatenate([h0 * d0 + h1 * d1, h0 * d1 - h1 * d0], 1)
-                cross = cross.reshape(blocks * 2 * SUB, width).astype(jnp.bfloat16)
-                y = jnp.dot(w1_ref[b], cross, preferred_element_type=jnp.float32)
-                y_ref[:, b] = y.astype(jnp.bfloat16).reshape(groups, 2 * SUB, width)
-            return norm
-
-        lax.fori_loop(0, lows, first_stage, 0)
+        @pl.loop(0, lows // chunk - 1)
+        def _(step):
+            for i in range(chunk):
+                transform(step * chunk + i)
+                expand(tile, (step + 1) * chunk + i)
+
+        @pl.when(tile + 1 < tiles)
+        def _():
+            arrive(tile + 1)
+
+        following = jnp.minimum(tile + 1, tiles - 1)
+        for i in range(chunk):
+            transform(lows - chunk + i)
+            expand(following, i)
 
         def add_squares(f, total):
             piece = recv_ref[tile, f].astype(jnp.float32).reshape(-1, SUB, LANES)
             return total + jnp.sum(piece * piece, 0)
 
-        norm = lax.fori_loop(0, parts, add_squares, jnp.zeros((SUB, LANES), jnp.float32))
+        norm = jnp.zeros((SUB, LANES), jnp.float32)
+        for f in range(parts):
+            norm = add_squares(f, norm)
         norm = jnp.dot(norm, collect, precision=lax.Precision.HIGHEST, preferred_element_type=jnp.float32)
         norm = jnp.sum(norm, 0, keepdims=True) * (SCALE * SCALE)
 
@@ -409,13 +440,18 @@
             z = jnp.dot(
                 w2_ref[...], y_ref[g].reshape(w2_ref.shape[1], width), preferred_element_type=jnp.float32
             )
-            half = z.shape[0] // 2
-            re, im = z[:half], z[half:]
-            power = (re * re + im * im).reshape(half // SUB, SUB, width)
-            return jnp.maximum(best, jnp.max(power, 0))
+            z = z.reshape(2, -1, SUB, width)
+            for t in range(RADIX // 2):
+                re, im = z[0, t], z[1, t]
+                if t + RADIX // 2 < z.shape[1]:
+                    inside = offset >= -(g * SUB + t * inner)
+                    re = jnp.where(inside, re, z[0, t + RADIX // 2])
+                    im = jnp.where(inside, im, z[1, t + RADIX // 2])
+                best = jnp.maximum(best, re * re + im * im)
+            return best
 
         best = lax.fori_loop(
-            0, groups, second_stage, jnp.zeros((SUB, width), jnp.float32), unroll=4
+            0, groups, second_stage, jnp.zeros((SUB, width), jnp.float32), unroll=32
         )
         peak_ref[me, tile] = jnp.max(best, 0, keepdims=True) / norm
 
@@ -444,40 +480,41 @@
     highs = RADIX // parts
     width = LANES // parts * segs
     base, turn, second = fused_tables(bins)
-    strain = spectra.reshape(halves, SUB, RADIX, 2, segs_here).transpose(4, 0, 2, 3, 1)
-    strain = strain.reshape(segs_here, 2 * bins_here)
     groups = 2 * bins // RADIX // SUB
-    anywhere = pl.BlockSpec(memory_space=pl.ANY)
+    far = pl.BlockSpec(memory_space=pltpu.HBM)
     whole = pl.BlockSpec(memory_space=pltpu.VMEM)
     dma = pltpu.SemaphoreType.DMA
     chunk = (halves, highs, 2 * SUB, LANES)
     out = pl.pallas_call(
         fused_kernel,
         out_shape=jax.ShapeDtypeStruct((parts, tiles, width), jnp.float32),
-        in_specs=[anywhere, whole, pl.BlockSpec(memory_space=pltpu.SMEM), anywhere, anywhere, anywhere],
+        in_specs=[far, far, pl.BlockSpec(memory_space=pltpu.SMEM), far, far, far],
         out_specs=whole,
         scratch_shapes=[
             pltpu.VMEM((tiles, bins_here, 2, LANES), jnp.bfloat16),
+            pltpu.VMEM((bins_here, 2, segs_here), jnp.bfloat16),
             pltpu.VMEM((tiles, parts) + chunk, jnp.bfloat16),
             pltpu.VMEM((tiles, parts) + chunk, jnp.bfloat16),
             pltpu.VMEM(base.shape, jnp.float32),
             pltpu.VMEM(turn.shape, jnp.float32),
             pltpu.VMEM(second.shape, jnp.bfloat16),
             pltpu.VMEM((RADIX, groups * 2 * SUB, 2 * bins // RADIX), jnp.bfloat16),
+            pltpu.VMEM((segs_here, 2 * bins_here), jnp.bfloat16),
             pltpu.VMEM((crowd, parts, segs_here, 2 * bins_here), jnp.bfloat16),
             pltpu.VMEM((RADIX, parts * halves, 2 * SUB, LANES), jnp.float32),
+            pltpu.VMEM((RADIX, 2 * bins // RADIX, width), jnp.bfloat16),
             pltpu.VMEM((groups, RADIX, 2 * SUB, width), jnp.bfloat16),
             pltpu.VMEM((parts, tiles, 1, width), jnp.float32),
-            dma((tiles,)), dma((3,)),
+            dma((tiles,)), dma((4,)),
             dma((tiles, parts)), dma((tiles, parts)),
             dma((parts,)), dma((parts,)),
             dma((crowd,)), dma((crowd,)),
             dma((parts,)), dma((parts,)),
         ],
         compiler_params=pltpu.CompilerParams(
-            vmem_limit_bytes=50 * 1024 * 1024, collective_id=0, has_side_effects=True
+            vmem_limit_bytes=60 * 1024 * 1024, collective_id=0, has_side_effects=True
         ),
-    )(templates, strain, valid_start, jnp.asarray(base), jnp.asarray(turn), jnp.asarray(second))
+    )(templates, spectra, valid_start, jnp.asarray(base), jnp.asarray(turn), jnp.asarray(second))
     return out.transpose(1, 0, 2).reshape(rows_here, segs)
 
 

time: 58.5 us -> 41.5 us (0.71)
  Pallas kernels: 52.5 us -> 38 us
  local copies, waits for them, and re-layouts: 5.58 us -> 3.25 us
    pallas_call x1, Pallas kernels: 52.5 us -> 38 us  [fused(): pl.pallas_call(fused_kernel, out_shape=jax.ShapeDtypeStruct((parts, tiles...]
    unnamed x10 -> x1, local copies, waits for them, and re-layouts: 3.67 us -> 1.5 us
    reshape x3 -> x0, local copies, waits for them, and re-layouts: 1 us -> none  [the longest x2 0.88 us: fused(): spectra.reshape(halves, SUB, RADIX, 2, segs_here).transpose(4, 0, 2, 3, 1)]
    transpose x1, local copies, waits for them, and re-layouts: 0.02 us -> 0.86 us  [fused(): return out.transpose(1, 0, 2).reshape(rows_here, segs)]
where the time goes in v2:
time: 41.5 us; the launch traced here: 41.3 us
  Pallas kernels  38 us (92%)
  local copies, waits for them, and re-layouts  3.25 us (8%)
    pallas_call x1, Pallas kernels, fused(): pl.pallas_call(fused_kernel, out_shape=jax.ShapeDtypeStruct((parts, tiles...  38 us
    unnamed x1, local copies, waits for them, and re-layouts  1.5 us
    reshape x2, local copies, waits for them, and re-layouts, fused(): return out.transpose(1, 0, 2).reshape(rows_here, segs)  0.89 us
    transpose x1, local copies, waits for them, and re-layouts, fused(): return out.transpose(1, 0, 2).reshape(rows_here, segs)  0.86 us

profile of v2, /device:TPU:0, one launch (start us, length us, event | category | flops | bytes accessed | tf_op | source)
XLA Modules:
  0.0 41.3 jit_solution(3709501730626035803)
XLA Ops:
  0.0 1.5 %copy.8.s_hbm = bf16[256,2,4]{2,1,0:T(2,128)(2,1)} copy(bf16[256,2,4]{0,2,1:T(4,128)(2,1)} %param.6) | data formatting | bytes 8192 | tf_op args[0]
  1.5 38.0 %shard_map.64 = f32[8,5,256]{2,1,0:T(8,128)} custom-call(bf16[256,2,640]{2,1,0:T(2,128)(2,1)} %x_hbm.1, bf16[256,2,4]{2,1,0:T(2,128)(2,1)} %copy.8.s_hbm, s32[16]{0:T(128)} %vs_ref.1, f32[32,2,8,256]{3,2,1,0:T(8,128)} %constant.6.clone.base_hbm, f32[2,32,8,1]{3,2,1,0:T(8,128)} %constant.7.clone.turn_hbm, bf16[192,256]{1,0:T(8,128)(2,1)} %constant.8.clone.w2_hbm), custom_call_target="tpu_custom_call" | custom-call | tf_op jit(solution)/shard_map/pallas_call | solution.py:488
  39.5 0.9 %copy.9 = f32[5,8,256]{2,1,0:T(8,128)S(1)} copy(f32[5,8,256]{2,0,1:T(8,128)} %bitcast.1) | data formatting | bytes 81920 | tf_op jit(solution)/shard_map/transpose | solution.py:518
  40.4 0.1 reshape.3
  40.5 0.8 %copy.10 = f32[640,16]{0,1:T(8,128)} copy(f32[640,16]{1,0:T(8,128)S(1)} %reshape.3) | data formatting | bytes 81920 | tf_op jit(solution)/shard_map/reshape | solution.py:518

commit v3 on v2

--- a/solution.py
+++ b/solution.py
@@ -217,10 +217,23 @@
     return rows
 
 
+def corner_turn(x, size):
+    row = lax.broadcasted_iota(jnp.int32, x.shape, 0)
+    block = lax.broadcasted_iota(jnp.int32, x.shape, 1) // size
+    step = SUB // 2
+    while step:
+        low, left = (row // step) % 2, (block // step) % 2
+        below = pltpu.roll(pltpu.roll(x, SUB - step, 0), size * step, 1)
+        above = pltpu.roll(pltpu.roll(x, step, 0), LANES - size * step, 1)
+        x = jnp.where(low == left, x, jnp.where(low == 0, below, above))
+        step //= 2
+    return x
+
+
 def fused_kernel(
     x_hbm, s_hbm, vs_ref, base_hbm, turn_hbm, w2_hbm, out_ref,
     x_ref, own_ref, send_ref, recv_ref, work_ref, turn_ref, w2_ref, w1_ref, s_ref, strain_ref, dexp_ref,
-    cross_ref, y_ref, peak_ref,
+    pick_ref, cross_ref, y_ref, peak_ref,
     load_sem, table_sem, send_sem, recv_sem, ssend_sem, srecv_sem, gsend_sem, grecv_sem, psend_sem, precv_sem,
 ):
     tiles, parts = recv_ref.shape[:2]
@@ -301,12 +314,27 @@
     table_copies[0].wait()
     for tile in range(tiles):
         load(tile).wait()
-    strain = own_ref[...].reshape(halves, rows, own_ref.shape[2])
-    strain = [
-        lax.dot_general(strain[h], sort, (((0,), (1,)), ((), ())), preferred_element_type=jnp.float32)
-        for h in range(halves)
-    ]
-    s_ref[...] = jnp.concatenate(strain, 1).astype(jnp.bfloat16)
+    place = lax.broadcasted_iota(jnp.int32, (rows, rows), 1)
+    origin = ((place // SUB) % 2 * SUB + place % SUB) * RADIX + place // (2 * SUB)
+    order = (lax.broadcasted_iota(jnp.int32, (rows, rows), 0) == origin).astype(jnp.bfloat16)
+    span = SUB * RADIX
+    strain = []
+    for h in range(halves):
+        piece = jnp.concatenate([own_ref[c, :, h * span : (h + 1) * span] for c in range(2)], 1)
+        strain.append(jnp.dot(piece, order, preferred_element_type=jnp.float32))
+    strain = jnp.concatenate(strain, 1)
+    lane = lax.broadcasted_iota(jnp.int32, strain.shape, 1)
+    row = lax.broadcasted_iota(jnp.int32, strain.shape, 0)
+    start = jnp.zeros(strain.shape, jnp.int32)
+    for s in range(strain.shape[0]):
+        start = jnp.where(row == s, vs_ref[team * strain.shape[0] + s], start)
+    turns = (start >= quarter).astype(jnp.int32) + (start >= 2 * quarter).astype(jnp.int32)
+    turns = (turns * (lane // (2 * SUB))) % 4
+    imaginary = (lane // SUB) % 2 == 1
+    wide = strain.shape[1]
+    swapped = jnp.where(imaginary, pltpu.roll(strain, SUB, 1), -pltpu.roll(strain, wide - SUB, 1))
+    strain = jnp.where(turns % 2 == 1, swapped, strain)
+    s_ref[...] = jnp.where(turns >= 2, -strain, strain).astype(jnp.bfloat16)
     for tile in range(tiles):
         x = x_ref[tile].reshape(halves, rows, LANES)
         x = jnp.stack([jnp.dot(sort, x[h], preferred_element_type=jnp.float32) for h in range(halves)])
@@ -325,6 +353,18 @@
     for tile in range(tiles):
         recv_ref[tile, me] = send_ref[tile, me]
 
+    bank_row = lax.broadcasted_iota(jnp.int32, (LANES, 2 * LANES), 0)
+    bank_lane = lax.broadcasted_iota(jnp.int32, (LANES, 2 * LANES), 1)
+    for pair in range(lows // 2):
+        wanted = (2 * pair + bank_lane // LANES) * size + bank_lane % size
+        pick_ref[pair] = (bank_row == wanted).astype(jnp.bfloat16)
+    collect = (bank_row % size == bank_lane % size).astype(jnp.float32)
+    seg = lax.broadcasted_iota(jnp.int32, (SUB, width), 1) // size
+    start = jnp.zeros((SUB, width), jnp.int32)
+    for s in range(segs):
+        start = jnp.where(seg == s, vs_ref[s], start)
+    offset = lax.broadcasted_iota(jnp.int32, (SUB, width), 0) - start % quarter
+
     for copy in table_copies[1:]:
         copy.wait()
 
@@ -343,59 +383,34 @@
     for source in others(crowd, team):
         team_copy(source, source).wait_recv()
 
-    seg = lax.broadcasted_iota(jnp.int32, (SUB, LANES), 1) % segs
-    start = jnp.zeros((SUB, LANES), jnp.int32)
-    for s in range(segs):
-        start = jnp.where(seg == s, vs_ref[s], start)
-    turns = (start >= quarter).astype(jnp.int32) + (start >= 2 * quarter).astype(jnp.int32)
-    rest = start - turns * quarter
-    step_cos = 1.0 - turns.astype(jnp.float32)
-    step_sin = (turns == 1).astype(jnp.float32)
-
-    spread = (
-        lax.broadcasted_iota(jnp.int32, (segs, LANES), 0)
-        == lax.broadcasted_iota(jnp.int32, (segs, LANES), 1) % segs
-    ).astype(jnp.bfloat16)
-    unit = (jnp.ones((SUB, LANES), jnp.float32), jnp.zeros((SUB, LANES), jnp.float32))
-    factors = [unit]
-    for b in range(1, 4):
-        c, s = factors[-1]
-        factors.append((c * step_cos - s * step_sin, c * step_sin + s * step_cos))
+    lane_seg = lax.broadcasted_iota(jnp.int32, (segs, width), 1) // size
+    spread = (lax.broadcasted_iota(jnp.int32, (segs, width), 0) == lane_seg).astype(jnp.bfloat16)
     for f in range(parts):
         piece = jnp.concatenate([strain_ref[g, f] for g in range(crowd)], 0)
         piece = lax.dot_general(
             piece, spread, (((0,), (0,)), ((), ())), preferred_element_type=jnp.float32
         )
-        piece = piece.reshape(halves, RADIX, 2, SUB, LANES)
+        piece = piece.reshape(halves, RADIX, 2 * SUB, width)
         for h in range(halves):
-            for b in range(RADIX):
-                c, s = factors[b % 4]
-                d0, d1 = piece[h, b, 0], piece[h, b, 1]
-                dexp_ref[b, f * halves + h, :SUB] = d0 * c - d1 * s
-                dexp_ref[b, f * halves + h, SUB:] = d0 * s + d1 * c
-
-    lane_template = lax.broadcasted_iota(jnp.int32, (LANES, width), 1) // segs
-    bank_row = lax.broadcasted_iota(jnp.int32, (LANES, width), 0)
-    collect = (bank_row % size == lane_template).astype(jnp.float32)
-    offset = lax.broadcasted_iota(jnp.int32, (SUB, LANES), 0) - rest
-    offset = jnp.concatenate([offset] * (width // LANES), 1)
-
-    def expand(tile, i):
-        pick = (bank_row == i * size + lane_template).astype(jnp.bfloat16)
-        for high in range(highs):
-            b = high * lows + i
-            piece = recv_ref[tile, :, :, high].reshape(blocks * 2 * SUB, LANES)
-            bank = jnp.dot(piece, pick, preferred_element_type=jnp.float32)
-            bank = bank.reshape(blocks, 2 * SUB, width)
-            h0, h1 = bank[:, :SUB], bank[:, SUB:]
-            d0, d1 = dexp_ref[b, :, :SUB], dexp_ref[b, :, SUB:]
-            d0 = jnp.concatenate([d0] * (width // LANES), 2)
-            d1 = jnp.concatenate([d1] * (width // LANES), 2)
-            cross = jnp.concatenate([h0 * d0 + h1 * d1, h0 * d1 - h1 * d0], 1)
-            cross_ref[b] = cross.reshape(blocks * 2 * SUB, width).astype(jnp.bfloat16)
-
-    def transform(i):
-        for high in range(highs):
+            dexp_ref[:, f * halves + h] = piece[h]
+
+    def expand(tile, high):
+        piece = recv_ref[tile, :, :, high].reshape(blocks * 2 * SUB, LANES)
+        for pair in range(lows // 2):
+            bank = jnp.dot(piece, pick_ref[pair], preferred_element_type=jnp.float32)
+            bank = bank.reshape(blocks, 2 * SUB, 2 * LANES)
+            for k in range(2):
+                b = high * lows + 2 * pair + k
+                h0 = bank[:, :SUB, k * LANES : (k + 1) * LANES]
+                h1 = bank[:, SUB:, k * LANES : (k + 1) * LANES]
+                for side in range(width // LANES):
+                    here = slice(side * LANES, (side + 1) * LANES)
+                    d0, d1 = dexp_ref[b, :, :SUB, here], dexp_ref[b, :, SUB:, here]
+                    cross = jnp.concatenate([h0 * d0 + h1 * d1, h0 * d1 - h1 * d0], 1)
+                    cross_ref[b, :, here] = cross.reshape(blocks * 2 * SUB, LANES).astype(jnp.bfloat16)
+
+    def transform(high):
+        for i in range(lows):
             b = high * lows + i
             y = jnp.dot(w1_ref[b], cross_ref[b], preferred_element_type=jnp.float32)
             y_ref[:, b] = y.astype(jnp.bfloat16).reshape(groups, 2 * SUB, width)
@@ -404,27 +419,13 @@
         for source in others(parts, me):
             bank_copy(tile, source, source).wait_recv()
 
-    chunk = 4
-    arrive(0)
-    for i in range(chunk):
-        expand(0, i)
 
     @pl.loop(0, tiles)
     def _(tile):
-        @pl.loop(0, lows // chunk - 1)
-        def _(step):
-            for i in range(chunk):
-                transform(step * chunk + i)
-                expand(tile, (step + 1) * chunk + i)
-
-        @pl.when(tile + 1 < tiles)
-        def _():
-            arrive(tile + 1)
-
-        following = jnp.minimum(tile + 1, tiles - 1)
-        for i in range(chunk):
-            transform(lows - chunk + i)
-            expand(following, i)
+        arrive(tile)
+        for high in range(highs):
+            expand(tile, high)
+            transform(high)
 
         def add_squares(f, total):
             piece = recv_ref[tile, f].astype(jnp.float32).reshape(-1, SUB, LANES)
@@ -459,7 +460,12 @@
         peak_copy(me, target).start()
     for source in others(parts, me):
         peak_copy(source, source).wait_recv()
-    out_ref[...] = peak_ref[...].reshape(out_ref.shape)
+    for tile in range(tiles):
+        peaks = jnp.concatenate([peak_ref[p, tile] for p in range(parts)], 0)
+        for side in range(width // LANES):
+            out_ref[side * SUB : (side + 1) * SUB, tile * LANES : (tile + 1) * LANES] = corner_turn(
+                peaks[:, side * LANES : (side + 1) * LANES], size
+            )
     for target in others(parts, me):
         peak_copy(me, target).wait_send()
         strain_copy(me, target).wait_send()
@@ -487,12 +493,12 @@
     chunk = (halves, highs, 2 * SUB, LANES)
     out = pl.pallas_call(
         fused_kernel,
-        out_shape=jax.ShapeDtypeStruct((parts, tiles, width), jnp.float32),
+        out_shape=jax.ShapeDtypeStruct((segs, rows_here), jnp.float32),
         in_specs=[far, far, pl.BlockSpec(memory_space=pltpu.SMEM), far, far, far],
         out_specs=whole,
         scratch_shapes=[
             pltpu.VMEM((tiles, bins_here, 2, LANES), jnp.bfloat16),
-            pltpu.VMEM((bins_here, 2, segs_here), jnp.bfloat16),
+            pltpu.VMEM((2, segs_here, bins_here), jnp.bfloat16),
             pltpu.VMEM((tiles, parts) + chunk, jnp.bfloat16),
             pltpu.VMEM((tiles, parts) + chunk, jnp.bfloat16),
             pltpu.VMEM(base.shape, jnp.float32),
@@ -501,7 +507,8 @@
             pltpu.VMEM((RADIX, groups * 2 * SUB, 2 * bins // RADIX), jnp.bfloat16),
             pltpu.VMEM((segs_here, 2 * bins_here), jnp.bfloat16),
             pltpu.VMEM((crowd, parts, segs_here, 2 * bins_here), jnp.bfloat16),
-            pltpu.VMEM((RADIX, parts * halves, 2 * SUB, LANES), jnp.float32),
+            pltpu.VMEM((RADIX, parts * halves, 2 * SUB, width), jnp.float32),
+            pltpu.VMEM((parts // 2, LANES, 2 * LANES), jnp.bfloat16),
             pltpu.VMEM((RADIX, 2 * bins // RADIX, width), jnp.bfloat16),
             pltpu.VMEM((groups, RADIX, 2 * SUB, width), jnp.bfloat16),
             pltpu.VMEM((parts, tiles, 1, width), jnp.float32),
@@ -514,8 +521,8 @@
         compiler_params=pltpu.CompilerParams(
             vmem_limit_bytes=60 * 1024 * 1024, collective_id=0, has_side_effects=True
         ),
-    )(templates, spectra, valid_start, jnp.asarray(base), jnp.asarray(turn), jnp.asarray(second))
-    return out.transpose(1, 0, 2).reshape(rows_here, segs)
+    )(templates, spectra.transpose(1, 2, 0), valid_start, jnp.asarray(base), jnp.asarray(turn), jnp.asarray(second))
+    return out.T
 
 
 def fits(spectra, templates):
@@ -523,8 +530,7 @@
     segs = spectra.shape[2] * lax.axis_size("group")
     bins_here, _, rows_here = templates.shape
     return (
-        parts > 1
-        and RADIX % parts == 0
+        parts == SUB
         and rows_here % LANES == 0
         and bins_here % (SUB * RADIX) == 0
         and LANES // parts * segs == 2 * LANES

time: 41.5 us -> 37.7 us (0.908)
  Pallas kernels: 38 us -> 36.1 us
  local copies, waits for them, and re-layouts: 3.25 us -> 1.4 us
    pallas_call x1, Pallas kernels: 38 us -> 36.1 us  [fused(): pl.pallas_call(fused_kernel, out_shape=jax.ShapeDtypeStruct((segs, rows_h...]
    reshape x2 -> x0, local copies, waits for them, and re-layouts: 0.89 us -> none  [fused(): return out.transpose(1, 0, 2).reshape(rows_here, segs)]
    transpose x1 -> x0, local copies, waits for them, and re-layouts: 0.86 us -> none  [fused(): return out.transpose(1, 0, 2).reshape(rows_here, segs)]
where the time goes in v3:
time: 37.7 us; the launch traced here: 37.5 us
  Pallas kernels  36.1 us (96%)
  local copies, waits for them, and re-layouts  1.4 us (4%)
    pallas_call x1, Pallas kernels, fused(): pl.pallas_call(fused_kernel, out_shape=jax.ShapeDtypeStruct((segs, rows_h...  36.1 us
    unnamed x1, local copies, waits for them, and re-layouts  1.4 us

profile of v3, /device:TPU:0, one launch (start us, length us, event | category | flops | bytes accessed | tf_op | source)
XLA Modules:
  0.0 37.5 jit_solution(9849543083359262036)
XLA Ops:
  0.0 36.1 %shard_map.64 = f32[16,640]{1,0:T(8,128)} custom-call(bf16[256,2,640]{2,1,0:T(2,128)(2,1)} %x_hbm.1, bf16[2,4,256]{2,1,0:T(4,128)(2,1)} %bitcast.3, s32[16]{0:T(128)} %vs_ref.1, f32[32,2,8,256]{3,2,1,0:T(8,128)} %constant.6.clone.base_hbm, f32[2,32,8,1]{3,2,1,0:T(8,128)} %constant.7.clone.turn_hbm, bf16[192,256]{1,0:T(8,128)(2,1)} %constant.8.clone.w2_hbm), custom_call_target="tpu_custom_call" | custom-call | tf_op jit(solution)/shard_map/pallas_call | solution.py:494
  36.1 1.4 %copy.8 = f32[640,16]{0,1:T(8,128)} copy(f32[640,16]{0,1:T(8,128)} %bitcast.2) | data formatting | bytes 81920

commit v4 on v3

--- a/solution.py
+++ b/solution.py
@@ -254,7 +254,8 @@
     team = lax.axis_index("group")
 
     def others(count, here):
-        return [lax.rem(here + hop, count) for hop in range(1, count)]
+        hops = sorted(range(1, count), key=lambda hop: (-min(hop, count - hop), hop))
+        return [lax.rem(here + hop, count) for hop in hops]
 
     def load(tile):
         return pltpu.make_async_copy(
@@ -394,24 +395,23 @@
         for h in range(halves):
             dexp_ref[:, f * halves + h] = piece[h]
 
-    def expand(tile, high):
+    def expand(tile, high, pair):
         piece = recv_ref[tile, :, :, high].reshape(blocks * 2 * SUB, LANES)
-        for pair in range(lows // 2):
-            bank = jnp.dot(piece, pick_ref[pair], preferred_element_type=jnp.float32)
-            bank = bank.reshape(blocks, 2 * SUB, 2 * LANES)
-            for k in range(2):
-                b = high * lows + 2 * pair + k
-                h0 = bank[:, :SUB, k * LANES : (k + 1) * LANES]
-                h1 = bank[:, SUB:, k * LANES : (k + 1) * LANES]
-                for side in range(width // LANES):
-                    here = slice(side * LANES, (side + 1) * LANES)
-                    d0, d1 = dexp_ref[b, :, :SUB, here], dexp_ref[b, :, SUB:, here]
-                    cross = jnp.concatenate([h0 * d0 + h1 * d1, h0 * d1 - h1 * d0], 1)
-                    cross_ref[b, :, here] = cross.reshape(blocks * 2 * SUB, LANES).astype(jnp.bfloat16)
-
-    def transform(high):
-        for i in range(lows):
-            b = high * lows + i
+        bank = jnp.dot(piece, pick_ref[pair], preferred_element_type=jnp.float32)
+        bank = bank.reshape(blocks, 2 * SUB, 2 * LANES)
+        for k in range(2):
+            b = high * lows + 2 * pair + k
+            h0 = bank[:, :SUB, k * LANES : (k + 1) * LANES]
+            h1 = bank[:, SUB:, k * LANES : (k + 1) * LANES]
+            for side in range(width // LANES):
+                here = slice(side * LANES, (side + 1) * LANES)
+                d0, d1 = dexp_ref[b, :, :SUB, here], dexp_ref[b, :, SUB:, here]
+                cross = jnp.concatenate([h0 * d0 + h1 * d1, h0 * d1 - h1 * d0], 1)
+                cross_ref[b, :, here] = cross.reshape(blocks * 2 * SUB, LANES).astype(jnp.bfloat16)
+
+    def transform(high, pair):
+        for k in range(2):
+            b = high * lows + 2 * pair + k
             y = jnp.dot(w1_ref[b], cross_ref[b], preferred_element_type=jnp.float32)
             y_ref[:, b] = y.astype(jnp.bfloat16).reshape(groups, 2 * SUB, width)
 
@@ -423,9 +423,12 @@
     @pl.loop(0, tiles)
     def _(tile):
         arrive(tile)
-        for high in range(highs):
-            expand(tile, high)
-            transform(high)
+        pairs = [(high, pair) for high in range(highs) for pair in range(lows // 2)]
+        expand(tile, *pairs[0])
+        for now, later in zip(pairs, pairs[1:] + [None]):
+            if later is not None:
+                expand(tile, *later)
+            transform(*now)
 
         def add_squares(f, total):
             piece = recv_ref[tile, f].astype(jnp.float32).reshape(-1, SUB, LANES)
@@ -458,6 +461,12 @@
 
     for target in others(parts, me):
         peak_copy(me, target).start()
+    for target in others(parts, me):
+        strain_copy(me, target).wait_send()
+        for tile in range(tiles):
+            bank_copy(tile, me, target).wait_send()
+    for target in others(crowd, team):
+        team_copy(team, target).wait_send()
     for source in others(parts, me):
         peak_copy(source, source).wait_recv()
     for tile in range(tiles):
@@ -468,11 +477,6 @@
             )
     for target in others(parts, me):
         peak_copy(me, target).wait_send()
-        strain_copy(me, target).wait_send()
-        for tile in range(tiles):
-            bank_copy(tile, me, target).wait_send()
-    for target in others(crowd, team):
-        team_copy(team, target).wait_send()
 
 
 def fused(spectra, templates, valid_start):
@@ -519,7 +523,7 @@
             dma((parts,)), dma((parts,)),
         ],
         compiler_params=pltpu.CompilerParams(
-            vmem_limit_bytes=60 * 1024 * 1024, collective_id=0, has_side_effects=True
+            vmem_limit_bytes=56 * 1024 * 1024, collective_id=0, has_side_effects=True
         ),
     )(templates, spectra.transpose(1, 2, 0), valid_start, jnp.asarray(base), jnp.asarray(turn), jnp.asarray(second))
     return out.T

time: 37.7 us -> 37.5 us (level)
  no operation moved by 1% of the time
where the time goes in v4:
time: 37.5 us; the launch traced here: 37.3 us
  Pallas kernels  35.9 us (96%)
  local copies, waits for them, and re-layouts  1.4 us (4%)
    pallas_call x1, Pallas kernels, fused(): pl.pallas_call(fused_kernel, out_shape=jax.ShapeDtypeStruct((segs, rows_h...  35.9 us
    unnamed x1, local copies, waits for them, and re-layouts  1.4 us

profile of v4, /device:TPU:0, one launch (start us, length us, event | category | flops | bytes accessed | tf_op | source)
XLA Modules:
  0.0 37.3 jit_solution(1611542469927648322)
XLA Ops:
  0.0 35.9 %shard_map.64 = f32[16,640]{1,0:T(8,128)} custom-call(bf16[256,2,640]{2,1,0:T(2,128)(2,1)} %x_hbm.1, bf16[2,4,256]{2,1,0:T(4,128)(2,1)} %bitcast.3, s32[16]{0:T(128)} %vs_ref.1, f32[32,2,8,256]{3,2,1,0:T(8,128)} %constant.6.clone.base_hbm, f32[2,32,8,1]{3,2,1,0:T(8,128)} %constant.7.clone.turn_hbm, bf16[192,256]{1,0:T(8,128)(2,1)} %constant.8.clone.w2_hbm), custom_call_target="tpu_custom_call" | custom-call | tf_op jit(solution)/shard_map/pallas_call | solution.py:498
  35.9 1.4 %copy.8 = f32[640,16]{0,1:T(8,128)} copy(f32[640,16]{0,1:T(8,128)} %bitcast.2) | data formatting | bytes 81920

commit v5 on v4

--- a/solution.py
+++ b/solution.py
@@ -13,6 +13,7 @@
 RADIX = 16
 SUB = 8
 SCALE = 1.1328125
+AHEAD = 3
 
 
 def rotation(angle, row_axis, col_axis):
@@ -347,7 +348,8 @@
     pl.semaphore_wait(barrier, parts + crowd - 2)
     for target in others(parts, me):
         strain_copy(me, target).start()
-    for tile in range(tiles):
+    ahead = min(AHEAD, tiles)
+    for tile in range(ahead):
         for target in others(parts, me):
             bank_copy(tile, me, target).start()
     strain_ref[team, me] = s_ref[...]
@@ -423,6 +425,12 @@
     @pl.loop(0, tiles)
     def _(tile):
         arrive(tile)
+
+        @pl.when(tile + ahead < tiles)
+        def _():
+            for target in others(parts, me):
+                bank_copy(tile + ahead, me, target).start()
+
         pairs = [(high, pair) for high in range(highs) for pair in range(lows // 2)]
         expand(tile, *pairs[0])
         for now, later in zip(pairs, pairs[1:] + [None]):

time: 37.5 us -> 37.6 us (level)
  no operation moved by 1% of the time
where the time goes in v5:
time: 37.6 us; the launch traced here: 37.4 us
  Pallas kernels  36 us (96%)
  local copies, waits for them, and re-layouts  1.4 us (4%)
    pallas_call x1, Pallas kernels, fused(): pl.pallas_call(fused_kernel, out_shape=jax.ShapeDtypeStruct((segs, rows_h...  36 us
    unnamed x1, local copies, waits for them, and re-layouts  1.4 us

profile of v5, /device:TPU:0, one launch (start us, length us, event | category | flops | bytes accessed | tf_op | source)
XLA Modules:
  0.0 37.4 jit_solution(16551399879605556687)
XLA Ops:
  0.0 36.0 %shard_map.64 = f32[16,640]{1,0:T(8,128)} custom-call(bf16[256,2,640]{2,1,0:T(2,128)(2,1)} %x_hbm.1, bf16[2,4,256]{2,1,0:T(4,128)(2,1)} %bitcast.3, s32[16]{0:T(128)} %vs_ref.1, f32[32,2,8,256]{3,2,1,0:T(8,128)} %constant.6.clone.base_hbm, f32[2,32,8,1]{3,2,1,0:T(8,128)} %constant.7.clone.turn_hbm, bf16[192,256]{1,0:T(8,128)(2,1)} %constant.8.clone.w2_hbm), custom_call_target="tpu_custom_call" | custom-call | tf_op jit(solution)/shard_map/pallas_call | solution.py:506
  36.0 1.4 %copy.8 = f32[640,16]{0,1:T(8,128)} copy(f32[640,16]{0,1:T(8,128)} %bitcast.2) | data formatting | bytes 81920

commit v6 on v5

--- a/solution.py
+++ b/solution.py
@@ -349,9 +349,8 @@
     for target in others(parts, me):
         strain_copy(me, target).start()
     ahead = min(AHEAD, tiles)
-    for tile in range(ahead):
-        for target in others(parts, me):
-            bank_copy(tile, me, target).start()
+    for target in others(parts, me):
+        bank_copy(0, me, target).start()
     strain_ref[team, me] = s_ref[...]
     for tile in range(tiles):
         recv_ref[tile, me] = send_ref[tile, me]
@@ -383,6 +382,9 @@
         strain_copy(source, source).wait_recv()
     for target in others(crowd, team):
         team_copy(team, target).start()
+    for tile in range(1, ahead):
+        for target in others(parts, me):
+            bank_copy(tile, me, target).start()
     for source in others(crowd, team):
         team_copy(source, source).wait_recv()
 

time: 37.6 us -> 37.6 us (level)
  no operation moved by 1% of the time
where the time goes in v6:
time: 37.6 us; the launch traced here: 37.4 us
  Pallas kernels  36 us (96%)
  local copies, waits for them, and re-layouts  1.4 us (4%)
    pallas_call x1, Pallas kernels, fused(): pl.pallas_call(fused_kernel, out_shape=jax.ShapeDtypeStruct((segs, rows_h...  36 us
    unnamed x1, local copies, waits for them, and re-layouts  1.4 us

profile of v6, /device:TPU:0, one launch (start us, length us, event | category | flops | bytes accessed | tf_op | source)
XLA Modules:
  0.0 37.4 jit_solution(7099716449294374050)
XLA Ops:
  0.0 36.0 %shard_map.64 = f32[16,640]{1,0:T(8,128)} custom-call(bf16[256,2,640]{2,1,0:T(2,128)(2,1)} %x_hbm.1, bf16[2,4,256]{2,1,0:T(4,128)(2,1)} %bitcast.3, s32[16]{0:T(128)} %vs_ref.1, f32[32,2,8,256]{3,2,1,0:T(8,128)} %constant.6.clone.base_hbm, f32[2,32,8,1]{3,2,1,0:T(8,128)} %constant.7.clone.turn_hbm, bf16[192,256]{1,0:T(8,128)(2,1)} %constant.8.clone.w2_hbm), custom_call_target="tpu_custom_call" | custom-call | tf_op jit(solution)/shard_map/pallas_call | solution.py:508
  36.0 1.4 %copy.8 = f32[640,16]{0,1:T(8,128)} copy(f32[640,16]{0,1:T(8,128)} %bitcast.2) | data formatting | bytes 81920
